TPU v7x, 32 devices: a whole 2x2x4 slice. The times are simulated.
32 devices in a mesh: ta: 2 (over core), gx: 16 (over z, y, x).
Axes of the slice: x: 2, y: 2, z: 4, core: 2. Of those that a mesh axis runs over, the one named last changes fastest.
Arguments:
- time_links: float32 [6, 2, 3, 3, 96, 4608], P('ta', None, None, None, 'gx'), may hold values from -1 to 1, as said below
Outputs:
- loop_planes: float32 [96, 2, 4608], P('gx', None, 'ta')
- correlator: float32 [96, 49], P('gx')
Inputs may be any that keep to these rules, and one draw needn't show every extreme that they name: At every site and time, the matrix time_links[t, 0] + i time_links[t, 1] is special unitary.
All inputs are finite; a program needn't handle non-finite values.
Results may differ from a plain program's by a relative error of at most 0.00029.
Values sent between devices are 32-bit elements; how exact they have to be, the bound alone decides.
A program may use at most 64 MiB of HBM per device.

v0:
```python
import jax
import jax.numpy as jnp
from jax import lax
from jax.sharding import PartitionSpec as P


def prefix(value, axis, join, neutral):
    count, mine = (lax.axis_size(axis), lax.axis_index(axis))
    pieces = lax.all_gather(value, axis)
    subtotal = jnp.full_like(value, 0) + jnp.asarray(neutral, value.dtype)

    def step(position, subtotal):
        longer = join(subtotal, pieces[position])
        return jnp.where(position < mine, longer, subtotal)

    return lax.fori_loop(0, count - 1, step, subtotal)


def spread(value, axis, source):
    kept = jnp.where(lax.axis_index(axis) == source, value, 0).astype(value.dtype)
    return lax.psum(kept, axis)


def complex_mul(left, right):
    terms_real = []
    terms_imag = []
    for middle in range(3):
        left_real = left[0][:, middle : middle + 1]
        left_imag = left[1][:, middle : middle + 1]
        right_real = right[0][middle : middle + 1]
        right_imag = right[1][middle : middle + 1]
        terms_real.append(left_real * right_real - left_imag * right_imag)
        terms_imag.append(left_real * right_imag + left_imag * right_real)
    return jnp.stack(
        [
            terms_real[0] + terms_real[1] + terms_real[2],
            terms_imag[0] + terms_imag[1] + terms_imag[2],
        ]
    )


def trace_third(matrix):
    return (matrix[:, 0, 0] + matrix[:, 1, 1] + matrix[:, 2, 2]) / 3.0


def correlation(own_rows, others):
    return lax.dot_general(
        own_rows,
        others,
        (((1,), (1,)), ((), ())),
        precision=lax.Precision.HIGHEST,
        preferred_element_type=jnp.float32,
    )


def by_separation(products, offset, longest, period):
    row_index = lax.broadcasted_iota(jnp.int32, products.shape, 0)
    column_index = lax.broadcasted_iota(jnp.int32, products.shape, 1)
    separation = offset + column_index - row_index
    separation = separation % period
    targets = jnp.arange(longest + 1, dtype=jnp.int32)
    selector = (separation[:, :, None] == targets).astype(jnp.float32)
    return jnp.sum(products[:, :, None] * selector, axis=1)


def per_device(time_links):
    local_product = time_links[0]
    for slice_index in range(1, time_links.shape[0]):
        local_product = complex_mul(local_product, time_links[slice_index])
    plane_sites = time_links.shape[-1]
    ta_count = lax.axis_size("ta")
    site_share = plane_sites // ta_count
    unit_matrix = jnp.broadcast_to(
        jnp.eye(3, dtype=jnp.float32)[:, :, None, None], local_product.shape[1:]
    )
    identity = jnp.stack([unit_matrix, jnp.zeros_like(unit_matrix)])
    earlier = prefix(local_product, "ta", complex_mul, identity)
    full_product = complex_mul(earlier, local_product)
    traces = spread(trace_third(full_product), "ta", ta_count - 1)
    own_share = lax.dynamic_slice_in_dim(traces, lax.axis_index("ta") * site_share, site_share, 2)
    loop_planes = jnp.transpose(own_share, (1, 0, 2))
    planes = loop_planes.shape[0]
    flat_width = loop_planes.shape[1] * loop_planes.shape[2]
    gx_count = lax.axis_size("gx")
    far_blocks = gx_count // 2
    longest = planes * far_blocks
    own_rows = loop_planes.reshape(planes, flat_width)
    shard_rows = lax.all_gather(loop_planes, "gx", axis=0, tiled=True)
    products = correlation(own_rows, shard_rows.reshape(shard_rows.shape[0], flat_width))
    totals_part = by_separation(
        products, -lax.axis_index("gx") * planes, longest, planes * gx_count
    )
    correlator = lax.psum(totals_part, "ta") / plane_sites
    return (loop_planes, correlator)


def solution(mesh):
    in_specs = (P("ta", None, None, None, "gx", None),)
    out_specs = (P("gx", None, "ta"), P("gx", None))
    return jax.shard_map(
        per_device, mesh=mesh, in_specs=in_specs, out_specs=out_specs, check_vma=False
    )
```

profile of v0, /device:TPU:0, one launch (start us, length us, event | category | flops | bytes accessed | tf_op | source)
XLA Modules:
  0.0 143.7 jit_solution(14677089066934302279)
XLA Ops:
  7.2 0.0 all-gather.6.cloned.1.call-start
  7.2 5.7 %fusion.13 = (f32[1,1,1,3,6,4608]{5,1,4,3,2,0:T(1,128)S(1)}, f32[1,1,1,3,6,4608]{5,1,4,3,2,0:T(1,128)S(1)}, f32[1,1,1,3,6,4608]{5,1,4,3,2,0:T(1,128)S(1)}, f32[1...) fusion(f32[3,2,3,3,6,4608]{5,1,4,3,2,0:T(2,128)} %param.1), kind=kLoop, calls=%fused_computation.88 | loop fusion | bytes 7962624 | tf_op jit(solution)/shard_map/slice | solution.py:30
  12.9 3.9 %fusion.14 = (f32[1,1,3,3,6,4608]{5,1,4,3,2,0:T(1,128)S(1)}, f32[1,1,3,3,6,4608]{5,1,4,3,2,0:T(1,128)S(1)}) fusion(f32[3,2,3,3,6,4608]{5,1,4,3,2,0:T(2,128)} %param.1), kind=kLoop, calls=%fused_computation.89 | loop fusion | bytes 3981312 | tf_op jit(solution)/shard_map/slice | solution.py:28
  16.9 0.3 copy_bitcast_fusion
  17.2 0.1 slice_bitcast_fusion.30
  17.3 0.1 slice_bitcast_fusion.31
  17.4 0.1 copy_bitcast_fusion.8
  17.5 0.1 copy_bitcast_fusion.10
  17.7 0.1 copy_bitcast_fusion.12
  17.8 1.0 subtract_add_fusion.4
  18.7 0.1 slice_bitcast_fusion.24
  18.8 0.0 copy-start.1
  18.8 0.1 slice_bitcast_fusion.25
  18.9 0.0 copy-start.2
  18.9 0.0 copy-start.3
  19.0 0.0 copy-start.4
  19.0 0.1 copy_bitcast_fusion.2
  19.1 0.1 copy_bitcast_fusion.4
  19.2 0.1 copy_bitcast_fusion.6
  19.3 0.3 copy-done.1
  19.7 0.1 copy-done.2
  19.8 0.1 copy-done.3
  19.9 0.2 copy-done.4
  20.1 0.9 subtract_add_fusion.3
  21.0 1.8 %pad_maximum_fusion = f32[2,3,3,6,4608]{4,3,2,1,0:T(8,128)} fusion(f32[1,3,3,6,4608]{4,3,2,1,0:T(8,128)S(1)} %get-tuple-element.56, f32[1,3,3,6,4608]{4,3,2,1,0:T(8,128)S(1)} %get-tuple-element.55), kind=kLoop, calls=%fused_computation | loop fusion | flops 497664 | bytes 3981312 | tf_op jit(solution)/shard_map/stack | solution.py:34
  22.8 0.0 all-gather.6.cloned.1.call-update
  22.8 0.2 all-reduce.3.cloned.1.call-start
  23.1 2.4 %subtract_add_fusion.1 = (f32[3,3,6,4608]{3,2,1,0:T(8,128)S(1)}, f32[3,3,6,4608]{3,2,1,0:T(8,128)S(1)}) fusion(f32[3,6,4608]{2,1,0:T(8,128)S(1)} %get-tuple-element.90, f32[3,6,4608]{2,1,0:T(8,128)S(1)} %get-tuple-element.77, f32[3,6,4608]{2,1,0:T(8,128)S(1)} %get-tuple-element.91, f32[3,6,4608]{2,1,0:T(8,128)} %copy-done.3, ...), kind=kLoop, calls=%fused_computation.11 | loop fusion | flops 5474304 | bytes 5971968 | tf_op jit(solution)/shard_map/add | solution.py:36
  25.5 0.1 slice_bitcast_fusion.10
  25.6 0.1 slice_bitcast_fusion.12
  25.7 15.4 %all-gather.6.cloned.1.call-done = f32[4,3,3,6,4608]{4,3,2,1,0:T(8,128)} async-done(((f32[2,3,3,6,4608]{4,3,2,1,0:T(8,128)}), f32[4,3,3,6,4608]{4,3,2,1,0:T(8,128)}) %all-gather.6.cloned.1.call-update) | async-done | bytes 3981328 | tf_op jit(solution)/shard_map/all_gather | solution.py:9
  41.0 0.0 copy-start
  41.0 2.1 %broadcast_multiply_fusion.5 = (f32[3,6,4608]{2,1,0:T(8,128)S(1)}, f32[3,6,4608]{2,1,0:T(8,128)S(1)}, f32[3,6,4608]{2,1,0:T(8,128)S(1)}, f32[3,6,4608]{2,1,0:T(8...) fusion(f32[2,2,3,3,6,4608]{5,4,3,2,1,0:T(8,128)} %bitcast.118), kind=kLoop, calls=%fused_computation.72 | loop fusion | flops 497664 | bytes 3981312 | tf_op jit(solution)/shard_map/while/body/eval_jaxpr/mul | solution.py:32
  43.1 1.2 copy-done
  44.3 0.2 slice_bitcast_fusion.19
  44.5 0.9 subtract_add_fusion.2
  45.4 0.2 stack_broadcast_in_dim.2
  45.5 0.3 maximum_select_fusion
  45.9 0.2 slice_bitcast_fusion.1
  46.1 0.1 slice_bitcast_fusion.11
  46.2 0.1 slice_bitcast_fusion.13
  46.3 1.0 subtract_add_fusion
  47.2 0.8 fusion.8
  48.0 0.0 all-reduce.3.cloned.1.call-update
  48.0 0.0 all-gather.4.cloned.1.call-start
  48.1 19.6 %all-reduce.3.cloned.1.call-done = f32[2,6,4608]{2,1,0:T(8,128)} async-done(((f32[2,6,4608]{2,1,0:T(8,128)}), f32[2,6,4608]{2,1,0:T(8,128)}) %all-reduce.3.cloned.1.call-update) | async-done | bytes 221200 | tf_op jit(solution)/shard_map/psum | solution.py:21
  67.7 0.9 dynamic-slice_bitcast_fusion
  68.6 0.7 copy.52
  69.3 0.0 all-gather.4.cloned.1.call-update
  69.3 61.6 %all-gather.4.cloned.1.call-done = f32[96,2,2304]{2,1,0:T(2,128)} async-done(((f32[6,2,2304]{2,1,0:T(2,128)}), f32[96,2,2304]{2,1,0:T(2,128)}) %all-gather.4.cloned.1.call-update) | async-done | bytes 1769488 | tf_op jit(solution)/shard_map/all_gather | solution.py:88
  131.0 2.9 %fusion.2 = f32[6,96]{1,0:T(8,128)S(1)} fusion(f32[6,2,2304]{2,0,1:T(8,128)S(1)} %dynamic-slice_bitcast_fusion, f32[96,2,2304]{2,1,0:T(2,128)} %all-gather.4.cloned.1.call-done), kind=kOutput, calls=%fused_computation.18 | convolution fusion | flops 31850496 | bytes 1882368 | tf_op jit(solution)/shard_map/dot_general | solution.py:47
  133.9 0.1 select_reduce_fusion
  134.1 2.5 %psum.15 = f32[6,49]{1,0:T(8,128)S(1)} all-reduce(f32[6,49]{1,0:T(8,128)S(1)} %select_reduce_fusion), channel_id=1, replica_groups=mesh['ta'=2,'gx'=16] {'ta'}, use_global_device_ids=true, to_apply=%region_2.3 | all-reduce | flops 294 | bytes 2352 | tf_op jit(solution)/shard_map/psum | solution.py:93
  136.5 0.6 broadcast_multiply_fusion.6
  (4 shorter events, 0.0 us)
Async XLA Ops:
  7.2 33.9 %all-gather.6.cloned.1.call-start = ((), (), s32[]{:S(2)}) async-start(), calls=%async_computation.2 | async-start | bytes 7962624 | tf_op jit(solution)/shard_map/all_gather | solution.py:9
  18.8 0.8 copy-start.1
  18.9 0.8 copy-start.2
  18.9 1.0 copy-start.3
  19.0 1.1 copy-start.4
  22.8 44.8 %all-reduce.3.cloned.1.call-start = ((), (), s32[]{:S(2)}) async-start(), calls=%async_computation | async-start | bytes 589824 | tf_op jit(solution)/shard_map/psum | solution.py:21
  41.0 3.3 %copy-start = (f32[4,3,3,6,4608]{4,3,2,1,0:T(8,128)S(1)}, f32[4,3,3,6,4608]{4,3,2,1,0:T(8,128)}, u32[]{:S(2)}) copy-start(f32[4,3,3,6,4608]{4,3,2,1,0:T(8,128)} %all-gather.6.cloned.1.call-done) | copy-start | bytes 11943940
  48.0 82.9 %all-gather.4.cloned.1.call-start = ((), (), s32[]{:S(2)}) async-start(), calls=%async_computation.1 | async-start | bytes 1880064 | tf_op jit(solution)/shard_map/all_gather | solution.py:88
Sparse Core Ops, SparseCore 0:
  22.9 18.0 all-gather.5
  48.2 19.4 all-reduce.2
  71.0 59.8 all-gather.3
where the time goes:
time: 144 us
  waiting for transfers between devices  96.6 us (67%)
  local copies, waits for them, and re-layouts  15.5 us (11%)
  between operations  14 us (10%)
  other arithmetic  11.8 us (8%)
  matrix products  2.94 us (2%)
  blocking collectives  2.47 us (2%)
    all_gather x1, waiting for transfers between devices, per_device(): shard_rows = lax.all_gather(loop_planes, 'gx', axis=0, tiled=True)  61.6 us
    psum x1, waiting for transfers between devices, spread(): return lax.psum(kept, axis)  19.6 us
    all_gather x1, waiting for transfers between devices, prefix(): pieces = lax.all_gather(value, axis)  15.4 us
    add x5, other arithmetic, complex_mul(): terms_real[0] + terms_real[1] + terms_real[2]  6.09 us
    slice x1, local copies, waits for them, and re-layouts, complex_mul(): right_real = right[0][middle:middle + 1]  5.72 us
    slice x2, local copies, waits for them, and re-layouts, complex_mul(): left_real = left[0][:, middle:middle + 1]  3.92 us
    dot_general x1, matrix products, correlation(): lax.dot_general(own_rows, others, (((1,), (1,)), ((), ())), precision=lax...  2.94 us
  transfers between devices with their start and end apart: 3, of which 3 were waited for; matrix products, arithmetic and copies ran while one was open for 2% of the time, Pallas kernels for 0%

commit v1 on v0

v1 whole, which is shorter than its diff:
```python
import functools

import jax
import jax.numpy as jnp
from jax import lax
from jax.experimental import pallas as pl
from jax.experimental.pallas import tpu as pltpu
from jax.sharding import PartitionSpec as P

LANES = 128
SUBLANES = 8
MESH = pl.DeviceIdType.MESH


def cross_conj(first, second):
    row = []
    for k in range(3):
        a, b = (k + 1) % 3, (k + 2) % 3
        ar, ai = first[a]
        br, bi = first[b]
        cr, ci = second[a]
        dr, di = second[b]
        real = (ar * dr - ai * di) - (br * cr - bi * ci)
        imag = (br * ci + bi * cr) - (ar * di + ai * dr)
        row.append((real, imag))
    return row


def row_times(row, matrix):
    out = []
    for k in range(3):
        real = imag = None
        for m in range(3):
            ar, ai = row[m]
            br, bi = matrix[m][k]
            pr = ar * br - ai * bi
            pi = ar * bi + ai * br
            real = pr if real is None else real + pr
            imag = pi if imag is None else imag + pi
        out.append((real, imag))
    return out


def product_rows(load, slices):
    rows = [[load(0, r, c) for c in range(3)] for r in range(2)]
    for t in range(1, slices):
        matrix = [[load(t, r, c) for c in range(3)] for r in range(2)]
        matrix.append(cross_conj(matrix[0], matrix[1]))
        rows = [row_times(row, matrix) for row in rows]
    return rows


def trace_of_product(left, right):
    left = left + [cross_conj(left[0], left[1])]
    right = right + [cross_conj(right[0], right[1])]
    real = imag = None
    for i in range(3):
        for j in range(3):
            ar, ai = left[i][j]
            br, bi = right[j][i]
            pr = ar * br - ai * bi
            pi = ar * bi + ai * br
            real = pr if real is None else real + pr
            imag = pi if imag is None else imag + pi
    return real / 3.0, imag / 3.0


def kernel(
    dims,
    x_ref,
    loop_ref,
    corr_ref,
    xin,
    psend,
    precv,
    tr,
    gath,
    gram,
    part,
    sel,
    in_sem,
    out_sem,
    s1,
    r1,
    s2,
    r2,
    s3,
    r3,
):
    slices, planes, sites, gx_n, chunks, reducers, longest = dims
    half = sites // 2
    chunk = half // chunks
    tiles = chunk // LANES
    per = 2 * half // LANES // reducers
    width = per * LANES
    rp = tr.shape[0]
    wide = gram.shape[1]
    ta = lax.axis_index("ta")
    gx = lax.axis_index("gx")
    other = 1 - ta
    mine = (gx * reducers + gx_n - 1) // gx_n
    is_reducer = jnp.logical_and(mine < reducers, (mine * gx_n) // reducers == gx)

    def in_copy(order, c):
        owner = other if order == 0 else ta
        start = pl.multiple_of(owner * half + c * chunk, LANES)
        slot = order * chunks + c
        return pltpu.make_async_copy(
            x_ref.at[:, pl.ds(0, 2), :, :, :, pl.ds(start, chunk)],
            xin.at[slot],
            in_sem.at[slot],
        )

    for order in range(2):
        for c in range(chunks):
            in_copy(order, c).start()

    barrier = pltpu.get_barrier_semaphore()
    for core in range(2):

        def greet(j, carry, core=core):
            @pl.when(jnp.logical_or(core != ta, j != gx))
            def _():
                pl.semaphore_signal(barrier, inc=1, device_id={"ta": core, "gx": j}, device_id_type=MESH)

            return carry

        lax.fori_loop(0, gx_n, greet, 0)

    tr[...] = jnp.zeros(tr.shape, jnp.float32)

    def loader(slot, lanes):
        def load(t, r, c):
            return tuple(xin[slot, t, r, c, :, q, lanes] for q in range(2))

        return load

    def far_chunk(c):
        in_copy(0, c).wait()
        slot = c

        def tile(i, carry):
            lanes = pl.ds(pl.multiple_of(i * LANES, LANES), LANES)
            rows = product_rows(loader(slot, lanes), slices)
            for r in range(2):
                for k in range(3):
                    for q in range(2):
                        psend[slot, (r * 3 + k) * 2 + q, 0:planes, lanes] = rows[r][k][q]
            return carry

        lax.fori_loop(0, tiles, tile, 0)

    for c in range(chunks):
        far_chunk(c)

    pl.semaphore_wait(barrier, 2 * gx_n - 1)

    def swap(c):
        return pltpu.make_async_remote_copy(
            src_ref=psend.at[c],
            dst_ref=precv.at[c],
            send_sem=s1.at[c],
            recv_sem=r1.at[c],
            device_id={"ta": other, "gx": gx},
            device_id_type=MESH,
        )

    for c in range(chunks):
        swap(c).start()

    def scatter(k, target, sender):
        return pltpu.make_async_remote_copy(
            src_ref=tr.at[:, pl.ds(pl.multiple_of(k * width, LANES), width)],
            dst_ref=gath.at[sender],
            send_sem=s2.at[k],
            recv_sem=r2.at[sender],
            device_id={"ta": ta, "gx": target},
            device_id_type=MESH,
        )

    def out_copy(c, q):
        lanes = pl.ds(pl.multiple_of(q * half + c * chunk, LANES), chunk)
        return pltpu.make_async_copy(
            tr.at[:, lanes],
            loop_ref.at[:, lanes],
            out_sem.at[c * 2 + q],
        )

    def near_chunk(step):
        c = step
        in_copy(1, c).wait()
        swap(c).wait_recv()

        def tile(i, carry):
            lanes = pl.ds(pl.multiple_of(i * LANES, LANES), LANES)
            rows = product_rows(loader(chunks + c, lanes), slices)
            theirs = [
                [
                    tuple(precv[c, (r * 3 + k) * 2 + q, 0:planes, lanes] for q in range(2))
                    for k in range(3)
                ]
                for r in range(2)
            ]
            pair = trace_of_product(rows, theirs)
            for q in range(2):
                place = pl.multiple_of(q * half + c * chunk + i * LANES, LANES)
                tr[0:planes, pl.ds(place, LANES)] = pair[q]
            return carry

        lax.fori_loop(0, tiles, tile, 0)
        for q in range(2):
            out_copy(c, q).start()
            for part_index in range(tiles // per):
                k = q * (reducers // 2) + c * (tiles // per) + part_index
                target = (k * gx_n) // reducers

                @pl.when(target != gx)
                def _():
                    scatter(k, target, gx).start()

                @pl.when(target == gx)
                def _():
                    lanes = pl.ds(pl.multiple_of(k * width, LANES), width)
                    gath[gx] = tr[:, lanes]

    for step in range(chunks):
        near_chunk(step)

    def select(i, carry):
        shape = (wide, sel.shape[2])
        column = lax.broadcasted_iota(jnp.int32, shape, 0)
        separation = lax.broadcasted_iota(jnp.int32, shape, 1)
        within = column % rp
        plane = planes * (column // rp) + within
        away = plane - (planes * gx + i + separation)
        hit = jnp.logical_or(away == 0, away == -planes * gx_n)
        hit = jnp.logical_and(hit, within < planes)
        sel[i] = jnp.where(hit, 1.0, 0.0).astype(jnp.bfloat16)
        return carry

    lax.fori_loop(0, planes, select, 0)

    def report(core, j, slot):
        return pltpu.make_async_remote_copy(
            src_ref=gram.at[pl.ds(pl.multiple_of(j * rp, SUBLANES), rp), :],
            dst_ref=part.at[slot],
            send_sem=s3.at[core * gx_n + j],
            recv_sem=r3.at[slot],
            device_id={"ta": core, "gx": j},
            device_id_type=MESH,
        )

    @pl.when(is_reducer)
    def _():
        def arrive(j, carry):
            @pl.when(j != gx)
            def _():
                scatter(0, gx, j).wait_recv()

            return carry

        lax.fori_loop(0, gx_n, arrive, 0)
        rows = gath[...].reshape(gx_n * rp, width)
        gram[...] = lax.dot_general(
            rows,
            rows,
            (((1,), (1,)), ((), ())),
            precision=lax.Precision.HIGHEST,
            preferred_element_type=jnp.float32,
        )
        slot = ta * reducers + mine
        for core in range(2):

            def tell(j, carry, core=core):
                @pl.when(jnp.logical_or(core != ta, j != gx))
                def _():
                    report(core, j, slot).start()

                return carry

            lax.fori_loop(0, gx_n, tell, 0)
        part[slot] = gram[pl.ds(pl.multiple_of(gx * rp, SUBLANES), rp), :]

    for core in range(2):

        def hear(k, carry, core=core):
            source = (k * gx_n) // reducers

            @pl.when(jnp.logical_or(core != ta, source != gx))
            def _():
                report(core, 0, core * reducers + k).wait_recv()

            return carry

        lax.fori_loop(0, reducers, hear, 0)

    total = jnp.sum(part[...], axis=0)
    high = total.astype(jnp.bfloat16).astype(jnp.float32)
    rest = total - high
    middle = rest.astype(jnp.bfloat16).astype(jnp.float32)
    low = rest - middle
    row_index = lax.broadcasted_iota(jnp.int32, total.shape, 0)
    answer = jnp.zeros((3 * rp, sel.shape[2]), jnp.float32)
    for i in range(planes):
        keep = row_index == i
        pieces = [jnp.where(keep, piece, 0.0) for piece in (high, middle, low)]
        stacked = jnp.concatenate(pieces, axis=0).astype(jnp.bfloat16)
        answer = answer + jnp.dot(stacked, sel[i], preferred_element_type=jnp.float32)
    answer = answer[0:rp] + answer[rp : 2 * rp] + answer[2 * rp : 3 * rp]
    corr_ref[...] = answer[0:planes, 0 : longest + 1] / sites

    for c in range(chunks):
        swap(c).wait_send()
        for q in range(2):
            out_copy(c, q).wait()

    def drain(k, carry):
        @pl.when((k * gx_n) // reducers != gx)
        def _():
            scatter(k, gx, gx).wait_send()

        return carry

    lax.fori_loop(0, reducers, drain, 0)

    @pl.when(is_reducer)
    def _():
        for core in range(2):

            def drain_report(j, carry, core=core):
                @pl.when(jnp.logical_or(core != ta, j != gx))
                def _():
                    report(core, j, 0).wait_send()

                return carry

            lax.fori_loop(0, gx_n, drain_report, 0)


def per_device(gx_n, time_links):
    slices, _, _, _, planes, sites = time_links.shape
    held = time_links.transpose(0, 2, 3, 4, 1, 5)
    half = sites // 2
    longest = planes * (gx_n // 2)
    blocks = half // LANES
    chunks = 3 if blocks % 3 == 0 else 1
    tiles = blocks // chunks
    per = min(p for p in range(1, tiles + 1) if tiles % p == 0 and 2 * blocks // p <= gx_n)
    reducers = 2 * blocks // per
    rp = -(-planes // SUBLANES) * SUBLANES
    wide = gx_n * rp
    chunk = tiles * LANES
    far = -(-(longest + 1) // LANES) * LANES
    dims = (slices, planes, sites, gx_n, chunks, reducers, longest)
    dma = pltpu.SemaphoreType.DMA
    loops, correlator = pl.pallas_call(
        functools.partial(kernel, dims),
        out_shape=(
            jax.ShapeDtypeStruct((rp, sites), jnp.float32),
            jax.ShapeDtypeStruct((planes, longest + 1), jnp.float32),
        ),
        in_specs=[pl.BlockSpec(memory_space=pl.ANY)],
        out_specs=(
            pl.BlockSpec(memory_space=pl.ANY),
            pl.BlockSpec(memory_space=pltpu.VMEM),
        ),
        scratch_shapes=[
            pltpu.VMEM((2 * chunks, slices, 2, 3, planes, 2, chunk), jnp.float32),
            pltpu.VMEM((chunks, 12, rp, chunk), jnp.float32),
            pltpu.VMEM((chunks, 12, rp, chunk), jnp.float32),
            pltpu.VMEM((rp, sites), jnp.float32),
            pltpu.VMEM((gx_n, rp, per * LANES), jnp.float32),
            pltpu.VMEM((wide, wide), jnp.float32),
            pltpu.VMEM((2 * reducers, rp, wide), jnp.float32),
            pltpu.VMEM((planes, wide, far), jnp.bfloat16),
            dma((2 * chunks,)),
            dma((2 * chunks,)),
            dma((chunks,)),
            dma((chunks,)),
            dma((reducers,)),
            dma((gx_n,)),
            dma((2 * gx_n,)),
            dma((2 * reducers,)),
        ],
        compiler_params=pltpu.CompilerParams(collective_id=0, has_side_effects=True),
    )(held)
    return loops[0:planes].reshape(planes, 2, half), correlator


def solution(mesh):
    in_specs = (P("ta", None, None, None, "gx", None),)
    out_specs = (P("gx", None, "ta"), P("gx", None))
    return jax.shard_map(
        functools.partial(per_device, mesh.shape["gx"]),
        mesh=mesh,
        in_specs=in_specs,
        out_specs=out_specs,
        check_vma=False,
    )
```

time: 144 us -> 35.9 us (0.25)
  waiting for transfers between devices: 96.6 us -> 0 us
  Pallas kernels: 0 us -> 31.9 us
  between operations: 14 us -> 0.64 us
  local copies, waits for them, and re-layouts: 15.5 us -> 2.89 us
  other arithmetic: 11.8 us -> 0 us
  matrix products: 2.94 us -> 0 us
  blocking collectives: 2.47 us -> 0 us
    all_gather x2 -> x0, waiting for transfers between devices: 77 us -> none  [the longest x1 61.6 us: per_device(): shard_rows = lax.all_gather(loop_planes, 'gx', axis=0, tiled=True)]
    pallas_call x0 -> x1, Pallas kernels: none -> 31.9 us  [per_device(): pl.pallas_call(functools.partial(kernel, dims), out_shape=(jax.ShapeDtype...]
    psum x1 -> x0, waiting for transfers between devices: 19.6 us -> none  [spread(): return lax.psum(kept, axis)]
    slice x3 -> x0, local copies, waits for them, and re-layouts: 9.64 us -> none  [the longest x1 5.72 us: complex_mul(): right_real = right[0][middle:middle + 1]]
    add x6 -> x0, other arithmetic: 6.1 us -> none  [the longest x5 6.09 us: complex_mul(): terms_real[0] + terms_real[1] + terms_real[2]]
    dot_general x1 -> x0, matrix products: 2.94 us -> none  [correlation(): lax.dot_general(own_rows, others, (((1,), (1,)), ((), ())), precision=lax...]
    psum x1 -> x0, blocking collectives: 2.47 us -> none  [per_device(): correlator = lax.psum(totals_part, 'ta') / plane_sites]
    mul x1 -> x0, other arithmetic: 2.11 us -> none  [complex_mul(): terms_real.append(left_real * right_real - left_imag * right_imag)]
  transfers between devices with their start and end apart: 3 -> 0, of which waited for: 3 -> 0; matrix products, arithmetic and copies ran while one was open for 2% -> 0% of each run, Pallas kernels for 0% -> 0%
where the time goes in v1:
time: 35.9 us; the launch traced here: 35.4 us
  Pallas kernels  31.9 us (89%)
  local copies, waits for them, and re-layouts  2.89 us (8%)
  between operations  0.64 us (2%)
    pallas_call x1, Pallas kernels, per_device(): pl.pallas_call(functools.partial(kernel, dims), out_shape=(jax.ShapeDtype...  31.9 us
    reshape x1, local copies, waits for them, and re-layouts, per_device(): return (loops[0:planes].reshape(planes, 2, half), correlator)  1.63 us
    unnamed x1, local copies, waits for them, and re-layouts  1.26 us

profile of v1, /device:TPU:0, one launch (start us, length us, event | category | flops | bytes accessed | tf_op | source)
XLA Modules:
  0.0 35.4 jit_solution(761569046716382325)
XLA Ops:
  0.6 31.9 %shard_map.30 = (f32[8,4608]{1,0:T(8,128)}, f32[6,49]{1,0:T(8,128)}) custom-call(f32[3,3,3,6,2,4608]{5,4,3,2,1,0:T(2,128)} %bitcast.2), custom_call_target="tpu_custom_call" | custom-call | tf_op jit(solution)/shard_map/pallas_call | solution.py:356
  32.5 1.6 %reshape.7 = f32[6,2,2304]{2,1,0:T(2,128)} reshape(f32[6,4608]{1,0:T(8,128)} %bitcast.3) | data formatting | bytes 221184 | tf_op jit(solution)/shard_map/reshape | solution.py:387
  34.2 1.3 %copy.4 = f32[6,49]{1,0:T(8,128)} copy(f32[6,49]{1,0:T(8,128)} %get-tuple-element.9) | data formatting | bytes 2352

commit v2 on v1

--- a/solution.py
+++ b/solution.py
@@ -101,19 +101,20 @@
     mine = (gx * reducers + gx_n - 1) // gx_n
     is_reducer = jnp.logical_and(mine < reducers, (mine * gx_n) // reducers == gx)
 
-    def in_copy(order, c):
+    def in_copy(order, c, i):
         owner = other if order == 0 else ta
-        start = pl.multiple_of(owner * half + c * chunk, LANES)
+        start = pl.multiple_of(owner * half + c * chunk + i * LANES, LANES)
         slot = order * chunks + c
         return pltpu.make_async_copy(
-            x_ref.at[:, pl.ds(0, 2), :, :, :, pl.ds(start, chunk)],
-            xin.at[slot],
-            in_sem.at[slot],
+            x_ref.at[:, pl.ds(0, 2), :, :, :, pl.ds(start, LANES)],
+            xin.at[slot, :, :, :, :, i],
+            in_sem.at[slot, i],
         )
 
     for order in range(2):
         for c in range(chunks):
-            in_copy(order, c).start()
+            for i in range(tiles):
+                in_copy(order, c, i).start()
 
     barrier = pltpu.get_barrier_semaphore()
     for core in range(2):
@@ -129,19 +130,25 @@
 
     tr[...] = jnp.zeros(tr.shape, jnp.float32)
 
-    def loader(slot, lanes):
+    flat = xin.reshape(*xin.shape[:4], planes * tiles * 2, LANES)
+
+    def loader(slot, i):
         def load(t, r, c):
-            return tuple(xin[slot, t, r, c, :, q, lanes] for q in range(2))
+            return tuple(
+                flat[slot, t, r, c, pl.ds(2 * i + q, planes, stride=2 * tiles), :]
+                for q in range(2)
+            )
 
         return load
 
     def far_chunk(c):
-        in_copy(0, c).wait()
+        for i in range(tiles):
+            in_copy(0, c, i).wait()
         slot = c
 
         def tile(i, carry):
             lanes = pl.ds(pl.multiple_of(i * LANES, LANES), LANES)
-            rows = product_rows(loader(slot, lanes), slices)
+            rows = product_rows(loader(slot, i), slices)
             for r in range(2):
                 for k in range(3):
                     for q in range(2):
@@ -188,12 +195,13 @@
 
     def near_chunk(step):
         c = step
-        in_copy(1, c).wait()
+        for i in range(tiles):
+            in_copy(1, c, i).wait()
         swap(c).wait_recv()
 
         def tile(i, carry):
             lanes = pl.ds(pl.multiple_of(i * LANES, LANES), LANES)
-            rows = product_rows(loader(chunks + c, lanes), slices)
+            rows = product_rows(loader(chunks + c, i), slices)
             theirs = [
                 [
                     tuple(precv[c, (r * 3 + k) * 2 + q, 0:planes, lanes] for q in range(2))
@@ -365,7 +373,7 @@
             pl.BlockSpec(memory_space=pltpu.VMEM),
         ),
         scratch_shapes=[
-            pltpu.VMEM((2 * chunks, slices, 2, 3, planes, 2, chunk), jnp.float32),
+            pltpu.VMEM((2 * chunks + 1, slices, 2, 3, planes, tiles, 2, LANES), jnp.float32),
             pltpu.VMEM((chunks, 12, rp, chunk), jnp.float32),
             pltpu.VMEM((chunks, 12, rp, chunk), jnp.float32),
             pltpu.VMEM((rp, sites), jnp.float32),
@@ -373,7 +381,7 @@
             pltpu.VMEM((wide, wide), jnp.float32),
             pltpu.VMEM((2 * reducers, rp, wide), jnp.float32),
             pltpu.VMEM((planes, wide, far), jnp.bfloat16),
-            dma((2 * chunks,)),
+            dma((2 * chunks, tiles)),
             dma((2 * chunks,)),
             dma((chunks,)),
             dma((chunks,)),

time: 35.9 us -> 25.8 us (0.72)
  Pallas kernels: 31.9 us -> 22.1 us
    pallas_call x1, Pallas kernels: 31.9 us -> 22.1 us  [per_device(): pl.pallas_call(functools.partial(kernel, dims), out_shape=(jax.ShapeDtype...]
where the time goes in v2:
time: 25.8 us; the launch traced here: 25.6 us
  Pallas kernels  22.1 us (86%)
  local copies, waits for them, and re-layouts  2.89 us (11%)
  between operations  0.64 us (2%)
    pallas_call x1, Pallas kernels, per_device(): pl.pallas_call(functools.partial(kernel, dims), out_shape=(jax.ShapeDtype...  22.1 us
    reshape x1, local copies, waits for them, and re-layouts, per_device(): return (loops[0:planes].reshape(planes, 2, half), correlator)  1.63 us
    unnamed x1, local copies, waits for them, and re-layouts  1.26 us

profile of v2, /device:TPU:0, one launch (start us, length us, event | category | flops | bytes accessed | tf_op | source)
XLA Modules:
  0.0 25.6 jit_solution(818105848694029471)
XLA Ops:
  0.6 22.1 %shard_map.30 = (f32[8,4608]{1,0:T(8,128)}, f32[6,49]{1,0:T(8,128)}) custom-call(f32[3,3,3,6,2,4608]{5,4,3,2,1,0:T(2,128)} %bitcast.2), custom_call_target="tpu_custom_call" | custom-call | tf_op jit(solution)/shard_map/pallas_call | solution.py:364
  22.7 1.6 %reshape.7 = f32[6,2,2304]{2,1,0:T(2,128)} reshape(f32[6,4608]{1,0:T(8,128)} %bitcast.3) | data formatting | bytes 221184 | tf_op jit(solution)/shard_map/reshape | solution.py:395
  24.3 1.3 %copy.4 = f32[6,49]{1,0:T(8,128)} copy(f32[6,49]{1,0:T(8,128)} %get-tuple-element.9) | data formatting | bytes 2352

commit v3 on v2

--- a/solution.py
+++ b/solution.py
@@ -351,7 +351,7 @@
     half = sites // 2
     longest = planes * (gx_n // 2)
     blocks = half // LANES
-    chunks = 3 if blocks % 3 == 0 else 1
+    chunks = next(c for c in (6, 3, 1) if blocks % c == 0)
     tiles = blocks // chunks
     per = min(p for p in range(1, tiles + 1) if tiles % p == 0 and 2 * blocks // p <= gx_n)
     reducers = 2 * blocks // per

time: 25.8 us -> 25.5 us (0.988)
  Pallas kernels: 22.1 us -> 21.8 us
    pallas_call x1, Pallas kernels: 22.1 us -> 21.8 us  [per_device(): pl.pallas_call(functools.partial(kernel, dims), out_shape=(jax.ShapeDtype...]
where the time goes in v3:
time: 25.5 us; the launch traced here: 25.3 us
  Pallas kernels  21.8 us (85%)
  local copies, waits for them, and re-layouts  2.89 us (11%)
  between operations  0.64 us (3%)
    pallas_call x1, Pallas kernels, per_device(): pl.pallas_call(functools.partial(kernel, dims), out_shape=(jax.ShapeDtype...  21.8 us
    reshape x1, local copies, waits for them, and re-layouts, per_device(): return (loops[0:planes].reshape(planes, 2, half), correlator)  1.63 us
    unnamed x1, local copies, waits for them, and re-layouts  1.26 us

profile of v3, /device:TPU:0, one launch (start us, length us, event | category | flops | bytes accessed | tf_op | source)
XLA Modules:
  0.0 25.3 jit_solution(6435602445348603375)
XLA Ops:
  0.6 21.8 %shard_map.30 = (f32[8,4608]{1,0:T(8,128)}, f32[6,49]{1,0:T(8,128)}) custom-call(f32[3,3,3,6,2,4608]{5,4,3,2,1,0:T(2,128)} %bitcast.2), custom_call_target="tpu_custom_call" | custom-call | tf_op jit(solution)/shard_map/pallas_call | solution.py:364
  22.4 1.6 %reshape.7 = f32[6,2,2304]{2,1,0:T(2,128)} reshape(f32[6,4608]{1,0:T(8,128)} %bitcast.3) | data formatting | bytes 221184 | tf_op jit(solution)/shard_map/reshape | solution.py:395
  24.0 1.3 %copy.4 = f32[6,49]{1,0:T(8,128)} copy(f32[6,49]{1,0:T(8,128)} %get-tuple-element.9) | data formatting | bytes 2352
